TPU v7x, 32 devices: a whole 2x2x4 slice. The times are simulated.
32 devices in a mesh: paths: 8 (over z, core), stocks: 4 (over y, x).
Axes of the slice: x: 2, y: 2, z: 4, core: 2. Of those that a mesh axis runs over, the one named last changes fastest.
Arguments:
- prices: bfloat16 [256, 131072], P('stocks', 'paths'), may hold values from -18 to 18
- loadings: bfloat16 [256, 32], P('stocks'), may hold values from -0.25 to 0.25
- basis_w: float32 [32, 512], replicated, may hold values from -1 to 1
- basis_bias: float32 [512], replicated, may hold values from -1 to 1
- payoff: bfloat16 [131072], P('paths'), may hold values from -4 to 4
- in_fit: int32 [131072], P('paths'), may hold values 0 or 1
- cotangent: bfloat16 [256, 131072], P('stocks', 'paths'), may hold values from -6 to 6
- shocks: bfloat16 [4, 256, 131072], P(None, 'stocks', 'paths'), may hold values from -6 to 6
- corr_gen: bfloat16 [256, 256], replicated, may hold values from -0.375 to 0.375
- basket: float32 [256], replicated, may hold values from 0.2 to 2
- exercise: int32 [4, 131072], P(None, 'paths'), may hold values 0 or 1
- bucket: int32 [4, 131072], P(None, 'paths'), may hold values from 0 to 255
Outputs:
- delta_out: float32 [256, 131072], P('stocks', 'paths')
- surface: float32 [256, 256], P('stocks', 'paths')
All inputs are finite; a program needn't handle non-finite values. No bound on the sum of `in_fit` or of `exercise` on one device may be relied on, other than what follows from the above.
Results may differ from a plain program's by a relative error of at most 0.003.
Values may be sent and summed in bfloat16 or wider, within the bound.
A program may use at most 192 MiB of HBM per device.

v0:
```python
import jax
import jax.numpy as jnp
from jax import lax
from jax.sharding import PartitionSpec as P

NK = 256
STEPS = 4


time_step = 0.25
ridge_weight = 0.1


def make_basis(factors, basis_w, basis_bias):
    raised = (
        jnp.dot(
            basis_w.T, factors, preferred_element_type=jnp.float32, precision=lax.Precision.HIGHEST
        )
        + basis_bias[:, None]
    )
    return jnp.tanh(raised).astype(jnp.bfloat16)


def regression_sums(basis, payoff, in_fit):
    picked = basis * in_fit.astype(jnp.bfloat16)[None, :]
    gram_sums = lax.dot_general(
        picked, basis, (((1,), (1,)), ((), ())), preferred_element_type=jnp.float32
    )
    moment = jnp.dot(picked, payoff, preferred_element_type=jnp.float32)
    return (gram_sums, moment)


def solve_coefficients(gram_sums, moment, path_count):
    system = gram_sums / path_count + ridge_weight * jnp.eye(gram_sums.shape[0], dtype=jnp.float32)
    cholesky_factor = jnp.linalg.cholesky(system)
    return jax.scipy.linalg.cho_solve((cholesky_factor, True), moment / path_count)


def per_device(
    prices,
    loadings,
    basis_w,
    basis_bias,
    payoff,
    in_fit,
    cotangent,
    shocks,
    corr_gen,
    basket,
    exercise,
    bucket,
):
    stock_count = lax.axis_size("stocks")
    local_paths = prices.shape[1]
    slab_part = local_paths // stock_count
    path_count = float(local_paths * lax.axis_size("paths"))
    offset = lax.axis_index("stocks") * slab_part
    partial_value = lax.dot_general(
        loadings, prices, (((0,), (0,)), ((), ())), preferred_element_type=jnp.float32
    )
    factors = lax.psum(partial_value, "stocks")
    basis = make_basis(factors, basis_w, basis_bias)
    gram_sums, moment = regression_sums(basis, payoff, in_fit)
    gram_sums, moment = lax.psum((gram_sums, moment), "paths")
    coefficients = solve_coefficients(gram_sums, moment, path_count)
    continuation = jnp.dot(
        coefficients, basis, preferred_element_type=jnp.float32, precision=lax.Precision.HIGHEST
    )
    continuation_own = lax.dynamic_slice_in_dim(continuation, offset, slab_part, 0)
    strikes = jnp.arange(NK, dtype=jnp.int32)
    stacked = jnp.concatenate([cotangent[None], shocks], axis=0)
    exchanged = lax.all_to_all(stacked, "stocks", split_axis=2, concat_axis=1, tiled=True)
    exercise_own = lax.dynamic_slice_in_dim(exercise, offset, slab_part, 1)
    bucket_own = lax.dynamic_slice_in_dim(bucket, offset, slab_part, 1)
    adjoint = exchanged[0].astype(jnp.float32)
    partial_surface = jnp.zeros((corr_gen.shape[0], NK), jnp.float32)
    for date_index in range(STEPS - 1, -1, -1):
        mixed_rows = jnp.dot(
            corr_gen, adjoint.astype(jnp.bfloat16), preferred_element_type=jnp.float32
        )
        adjoint = (
            adjoint
            + time_step * mixed_rows
            + exercise_own[date_index].astype(jnp.float32)[None, :]
            * continuation_own[None, :]
            * basket[:, None]
        )
        vega_terms = (adjoint * exchanged[date_index + 1].astype(jnp.float32)).astype(jnp.bfloat16)
        one_hot = (bucket_own[date_index][:, None] == strikes[None, :]).astype(jnp.bfloat16)
        partial_surface = partial_surface + jnp.dot(
            vega_terms, one_hot, preferred_element_type=jnp.float32
        )
    strike_share = lax.psum_scatter(partial_surface, "paths", scatter_dimension=1, tiled=True)
    surface = lax.psum_scatter(strike_share, "stocks", scatter_dimension=0, tiled=True)
    delta_out = lax.all_to_all(adjoint, "stocks", split_axis=0, concat_axis=1, tiled=True)
    return (delta_out, surface)


def solution(mesh):
    return jax.shard_map(
        per_device,
        mesh=mesh,
        in_specs=(
            P("stocks", "paths"),
            P("stocks", None),
            P(),
            P(),
            P("paths"),
            P("paths"),
            P("stocks", "paths"),
            P(None, "stocks", "paths"),
            P(),
            P(),
            P(None, "paths"),
            P(None, "paths"),
        ),
        out_specs=(P("stocks", "paths"), P("stocks", "paths")),
        check_vma=False,
    )
```

profile of v0, /device:TPU:0, one launch (start us, length us, event | category | flops | bytes accessed | tf_op | source)
XLA Modules:
  0.0 542.1 jit_solution(15361697601806816231)
XLA Ops:
  8.8 2.4 fusion.112
  11.2 9.7 %pad_maximum_fusion = bf16[5,64,16384]{2,1,0:T(8,128)(2,1)} fusion(bf16[4,64,16384]{2,1,0:T(8,128)(2,1)} %param.19, bf16[1,64,16384]{2,1,0:T(8,128)(2,1)} %bitcast.216), kind=kLoop, calls=%fused_computation.8 | loop fusion | flops 5242880 | bytes 20971520 | tf_op jit(solution)/shard_map/concatenate | solution.py:71
  20.9 33.2 %copy.54 = bf16[5,64,16384]{1,0,2:T(8,128)(2,1)} copy(bf16[5,64,16384]{2,1,0:T(8,128)(2,1)} %pad_maximum_fusion) | data formatting | bytes 20971520 | tf_op jit(solution)/shard_map/concatenate | solution.py:71
  54.1 39.6 %reshape.214 = bf16[4,2,655360]{2,1,0:T(2,128)(2,1)} reshape(bf16[16384,5,64]{2,1,0:T(8,128)(2,1)} %bitcast.206) | data formatting | bytes 20971520
  93.7 6.1 %all-to-all-start = ((bf16[4,2,655360]{2,1,0:T(2,128)(2,1)}), bf16[4,2,655360]{2,1,0:T(2,128)(2,1)}, u32[]{:S(2)}, u32[]{:S(2)}) async-start(bf16[4,2,655360]{2,1,0:T(2,128)(2,1)} %reshape.214), calls=%async_computation | async-start | bytes 20971520 | tf_op jit(solution)/shard_map/all_to_all | solution.py:72
  101.6 29.1 %tanh_convert_fusion = bf16[16384,512]{1,0:T(8,128)(2,1)S(1)} fusion(f32[32,16384]{1,0:T(8,128)} %all-reduce.4.cloned.1.call-done, f32[32,512]{1,0:T(8,128)S(1)} %copy-done.17, f32[512]{0:T(512)S(1)} %copy-done.18), kind=kOutput, calls=%fused_computation.2 | convolution fusion | flops 3238002688 | bytes 18941952 | tf_op jit(solution)/shard_map/dot_general | solution.py:16
  130.6 5.7 %copy-done.8 = bf16[16384,512]{1,0:T(8,128)(2,1)} copy-done((bf16[16384,512]{1,0:T(8,128)(2,1)}, bf16[16384,512]{1,0:T(8,128)(2,1)S(1)}, u32[]{:S(2)}) %copy-start.8) | copy-done | bytes 16777240
  136.4 14.0 %fusion.3 = f32[512,512]{0,1:T(8,128)} fusion(bf16[16384,512]{1,0:T(8,128)(2,1)S(1)} %tanh_convert_fusion, bf16[16384]{0:T(1024)(128)(2,1)S(1)} %convert_element_type.92), kind=kOutput, calls=%fused_computation.7 | convolution fusion | flops 8598323200 | bytes 17858560 | tf_op jit(solution)/shard_map/dot_general | solution.py:26
  150.4 11.1 %fusion.2 = f32[1,512]{1,0:T(1,128)S(1)} fusion(bf16[16384,1]{0,1:T(2,128)(2,1)S(1)} %reshape.178, bf16[16384,512]{1,0:T(8,128)(2,1)} %copy-done.8, bf16[16384]{0:T(1024)(128)(2,1)S(1)} %convert_element_type.92), kind=kOutput, calls=%fused_computation.6 | convolution fusion | flops 25165824 | bytes 16844800 | tf_op jit(solution)/shard_map/dot_general | solution.py:29
  161.4 18.5 %psum.23 = f32[512]{0:T(512)S(1)} all-reduce(f32[512]{0:T(512)S(1)} %bitcast.231), channel_id=1, replica_groups=mesh['paths'=8,'stocks'=4] {'paths'}, use_global_device_ids=true, to_apply=%region_10.11 | all-reduce | flops 512 | bytes 4096 | tf_op jit(solution)/shard_map/psum | solution.py:64
  180.0 32.8 %all-reduce.6.cloned.1.call-done = f32[512,512]{0,1:T(8,128)} async-done(((f32[512,512]{0,1:T(8,128)}), f32[512,512]{0,1:T(8,128)}) %all-reduce.6.cloned.1.call-update) | async-done | bytes 1048592 | tf_op jit(solution)/shard_map/psum | solution.py:64
  214.8 11.7 %cholesky.103 = f32[128,128]{1,0:T(8,128)S(1)} custom-call(f32[128,128]{1,0:T(8,128)S(1)} %cholesky.263), custom_call_target="Cholesky" | custom-call | tf_op jit(solution)/shard_map/jit(cholesky)/cholesky | solution.py:35
  226.5 9.8 %custom-call.34 = f32[1,128,128]{1,2,0:T(8,128)S(1)} custom-call(f32[1,128,128]{2,1,0:T(8,128)S(1)} %get-tuple-element.58), custom_call_target="InvertDiagBlocksLowerTriangular" | custom-call | tf_op jit(solution)/shard_map/jit(cholesky)/cholesky | solution.py:35
  237.3 11.7 %cholesky.215 = f32[128,128]{1,0:T(8,128)S(1)} custom-call(f32[128,128]{1,0:T(8,128)S(1)} %cholesky.267), custom_call_target="Cholesky" | custom-call | tf_op jit(solution)/shard_map/jit(cholesky)/cholesky | solution.py:35
  249.1 9.9 %custom-call.35 = f32[1,128,128]{1,2,0:T(8,128)S(1)} custom-call(f32[1,128,128]{2,1,0:T(8,128)S(1)} %get-tuple-element.56), custom_call_target="InvertDiagBlocksLowerTriangular" | custom-call | tf_op jit(solution)/shard_map/jit(cholesky)/cholesky | solution.py:35
  260.2 11.7 %cholesky.236 = f32[128,128]{1,0:T(8,128)S(1)} custom-call(f32[128,128]{1,0:T(8,128)S(1)} %cholesky.272), custom_call_target="Cholesky" | custom-call | tf_op jit(solution)/shard_map/jit(cholesky)/cholesky | solution.py:35
  272.0 9.8 %custom-call.36 = f32[1,128,128]{1,2,0:T(8,128)S(1)} custom-call(f32[1,128,128]{2,1,0:T(8,128)S(1)} %get-tuple-element.54), custom_call_target="InvertDiagBlocksLowerTriangular" | custom-call | tf_op jit(solution)/shard_map/jit(cholesky)/cholesky | solution.py:35
  282.6 11.9 %cholesky.253 = f32[128,128]{1,0:T(8,128)S(1)} custom-call(f32[128,128]{1,0:T(8,128)S(1)} %convolution_subtract_fusion.2), custom_call_target="Cholesky" | custom-call | tf_op jit(solution)/shard_map/jit(cholesky)/cholesky | solution.py:35
  299.5 8.9 %while.1 = (s32[]{:T(128)}, f32[512,512]{0,1:T(8,128)S(1)}, s32[4,2]{0,1:T(2,128)S(1)}, f32[4,128,128]{2,1,0:T(8,128)S(1)}, s32[]{:T(128)}) while((s32[]{:T(128)}, f32[512,512]{0,1:T(8,128)S(1)}, s32[4,2]{0,1:T(2,128)S(1)}, f32[4,128,128]{2,1,0:T(8,128)S(1)}, s32[]{:T(128)}) %tuple.48), condition=%wide.while_cond, body=%wide.while_body.sunk | while | flops 2 | bytes 393329 | solution.py:36
  308.4 39.3 %custom-call.37 = f32[4,128,128]{1,2,0:T(8,128)S(1)} custom-call(f32[4,128,128]{2,1,0:T(8,128)S(1)} %get-tuple-element.9), custom_call_target="InvertDiagBlocksLowerTriangular" | custom-call | tf_op jit(solution)/shard_map/jit(_cho_solve)/triangular_solve | solution.py:36
  350.6 16.6 %fusion = f32[1,16384]{1,0:T(1,128)S(1)} fusion(bf16[16384,512]{1,0:T(8,128)(2,1)} %copy-done.8, f32[128,1]{0,1:T(1,128)S(1)} %convolution_bitcast_fusion.5, f32[128,1]{0,1:T(1,128)S(1)} %convolution_bitcast_fusion.3, f32[128,1]{0,1:T(1,128)S(1)} %convolution_bitcast_fusion.1, f32[128,1]{0,1:T(1,128)S(1)} %convolution_bitcast_fusion), kind=kOutput, calls=%fused_computation.3 | convolution fusion | flops 100664832 | bytes 16844800 | tf_op jit(solution)/shard_map/dot_general | solution.py:66
  367.3 41.4 %reshape.215 = bf16[16384,5,64]{2,1,0:T(8,128)(2,1)} reshape(bf16[4,2,655360]{2,1,0:T(2,128)(2,1)} %all-to-all-done) | data formatting | bytes 20971520
  408.7 32.0 %copy.55 = bf16[5,64,4,4096]{3,1,2,0:T(8,128)(2,1)} copy(bf16[5,64,4,4096]{1,0,3,2:T(8,128)(2,1)} %bitcast.207) | data formatting | bytes 20971520 | tf_op jit(solution)/shard_map/all_to_all | solution.py:72
  440.6 7.0 %fusion.111 = (bf16[1,4,64,4096]{3,2,1,0:T(8,128)(2,1)}, bf16[1,4,64,4096]{3,2,1,0:T(8,128)(2,1)}, bf16[1,4,64,4096]{3,2,1,0:T(8,128)(2,1)}, bf16[1,4,64,4096]{3,2,1,0:T(8,128)(2,1)S(1)}, bf16[1,4,64,4096]{3,2,1,0:T(8,128)(2,1)S(1)}) fusion(bf16[5,4,64,4096]{3,2,1,0:T(8,128)(2,1)} %bitcast.208), kind=kLoop, calls=%fused_computation.171 | loop fusion | bytes 20971520 | tf_op jit(solution)/shard_map/slice | solution.py:88
  452.7 3.4 fusion.8
  456.0 4.8 all-to-all-start.1
  461.0 5.0 fusion.22
  466.0 1.9 fusion.43
  470.9 2.6 fusion.37
  473.6 30.4 %reduce-scatter.5.cloned.1.call-done = f32[256,32]{0,1:T(8,128)} async-done(((f32[256,256]{0,1:T(8,128)}), f32[256,32]{0,1:T(8,128)}) %reduce-scatter.5.cloned.1.call-update) | async-done | bytes 32784 | tf_op jit(solution)/shard_map/reduce_scatter | solution.py:93
  505.5 23.4 %reduce-scatter.7.cloned.1.call-done = f32[64,32]{1,0:T(8,128)} async-done(((f32[256,32]{1,0:T(8,128)}), f32[64,32]{1,0:T(8,128)}) %reduce-scatter.7.cloned.1.call-update) | async-done | bytes 8208
  530.3 4.8 copy.73
  (126 shorter events, 33.3 us)
Async XLA Ops:
  7.2 1.6 copy-start
  7.2 94.4 %all-reduce.4.cloned.1.call-start = ((), (), s32[]{:S(2)}) async-start(), calls=%async_computation.4 | async-start | bytes 4194304 | tf_op jit(solution)/shard_map/psum | solution.py:61
  93.7 6.4 %copy-start.14 = (s32[16384]{0:T(1024)S(1)}, s32[16384]{0:T(1024)}, u32[]{:S(2)}) copy-start(s32[16384]{0:T(1024)} %param.17) | copy-start | bytes 196612
  93.7 6.4 %copy-start.16 = (bf16[16384]{0:T(1024)(128)(2,1)S(1)}, bf16[16384]{0:T(1024)(128)(2,1)}, u32[]{:S(2)}) copy-start(bf16[16384]{0:T(1024)(128)(2,1)} %param.16) | copy-start | bytes 98308
  93.7 7.9 %copy-start.17 = (f32[32,512]{1,0:T(8,128)S(1)}, f32[32,512]{1,0:T(8,128)}, u32[]{:S(2)}) copy-start(f32[32,512]{1,0:T(8,128)} %param.14) | copy-start | bytes 196612
  93.7 7.9 %copy-start.18 = (f32[512]{0:T(512)S(1)}, f32[512]{0:T(512)}, u32[]{:S(2)}) copy-start(f32[512]{0:T(512)} %param.15) | copy-start | bytes 6148
  93.7 273.6 %all-to-all-start = ((bf16[4,2,655360]{2,1,0:T(2,128)(2,1)}), bf16[4,2,655360]{2,1,0:T(2,128)(2,1)}, u32[]{:S(2)}, u32[]{:S(2)}) async-start(bf16[4,2,655360]{2,1,0:T(2,128)(2,1)} %reshape.214), calls=%async_computation | async-start | bytes 20971520 | tf_op jit(solution)/shard_map/all_to_all | solution.py:72
  99.8 113.0 %all-reduce.6.cloned.1.call-start = ((), (), s32[]{:S(2)}) async-start(), calls=%async_computation.5 | async-start | bytes 2097152 | tf_op jit(solution)/shard_map/psum | solution.py:64
  130.6 5.7 %copy-start.8 = (bf16[16384,512]{1,0:T(8,128)(2,1)}, bf16[16384,512]{1,0:T(8,128)(2,1)S(1)}, u32[]{:S(2)}) copy-start(bf16[16384,512]{1,0:T(8,128)(2,1)S(1)} %tanh_convert_fusion) | copy-start | bytes 50331652
  212.7 1.8 copy-start.12
  440.6 7.0 %copy-start.13 = (bf16[256,256]{1,0:T(8,128)(2,1)S(1)}, bf16[256,256]{1,0:T(8,128)(2,1)}, u32[]{:S(2)}) copy-start(bf16[256,256]{1,0:T(8,128)(2,1)} %param.20) | copy-start | bytes 393220
  440.6 7.0 %copy-start.15 = (f32[256]{0:T(256)S(1)}, f32[256]{0:T(256)}, u32[]{:S(2)}) copy-start(f32[256]{0:T(256)} %param.21) | copy-start | bytes 3076
  448.8 2.0 copy-start.2
  450.7 1.9 copy-start.6
  452.7 3.4 copy-start.4
  456.0 74.3 %all-to-all-start.1 = ((f32[4,64,4096]{2,1,0:T(8,128)}), f32[4,64,4096]{2,1,0:T(8,128)}, u32[]{:S(2)}, u32[]{:S(2)}) async-start(f32[4,64,4096]{2,1,0:T(8,128)} %bitcast.209), calls=%async_computation.1 | async-start | bytes 8388608 | tf_op jit(solution)/shard_map/all_to_all | solution.py:95
  460.9 43.1 %reduce-scatter.5.cloned.1.call-start = ((), (), s32[]{:S(2)}) async-start(), calls=%async_computation.6 | async-start | bytes 294912 | tf_op jit(solution)/shard_map/reduce_scatter | solution.py:93
  461.0 5.0 copy-start.7
  461.0 5.0 copy-start.11
  466.0 2.2 copy-start.5
  466.0 2.9 copy-start.10
  467.9 2.8 copy-start.3
  467.9 3.0 copy-start.9
  473.6 55.3 %reduce-scatter.7.cloned.1.call-start = ((), (), s32[]{:S(2)}) async-start(), calls=%async_computation.7 | async-start | bytes 163840
  530.3 4.8 copy-start.1
Sparse Core Ops, SparseCore 0:
  11.7 72.1 all-reduce.3
  150.5 62.1 all-reduce.5
  473.7 30.2 reduce-scatter.4
  506.6 22.2 reduce-scatter.6
where the time goes:
time: 550 us; the launch traced here: 542 us
  local copies, waits for them, and re-layouts  181 us (33%)
  other arithmetic  131 us (24%)
  matrix products  96.1 us (17%)
  waiting for transfers between devices  86.6 us (16%)
  blocking collectives  18.5 us (3%)
  between operations  17.4 us (3%)
  starting transfers between devices  11.3 us (2%)
    unnamed x43, local copies, waits for them, and re-layouts  94.4 us
    another operation x14, other arithmetic, solve_coefficients(): cholesky_factor = jnp.linalg.cholesky(system)  78.7 us
    another operation x3, other arithmetic, solve_coefficients(): jax.scipy.linalg.cho_solve((cholesky_factor, True), moment / path_count)  39.5 us
    concatenate x1, local copies, waits for them, and re-layouts, per_device(): stacked = jnp.concatenate([cotangent[None], shocks], axis=0)  33.2 us
    psum x1, waiting for transfers between devices, per_device(): gram_sums, moment = lax.psum((gram_sums, moment), 'paths')  32.8 us
    all_to_all x1, local copies, waits for them, and re-layouts, per_device(): lax.all_to_all(stacked, 'stocks', split_axis=2, concat_axis=1, tiled=True)  32 us
    reduce_scatter x1, waiting for transfers between devices, per_device(): lax.psum_scatter(partial_surface, 'paths', scatter_dimension=1, tiled=True)  30.4 us
    dot_general x1, matrix products, make_basis(): jnp.dot(basis_w.T, factors, preferred_element_type=jnp.float32, precision...  29.1 us
  transfers between devices with their start and end apart: 6, of which 3 were waited for; matrix products, arithmetic and copies ran while one was open for 56% of the time, Pallas kernels for 0%

commit v1 on v0

v1 whole, which is shorter than its diff:
```python
import functools

import jax
import jax.numpy as jnp
from jax import lax
from jax.experimental import pallas as pl
from jax.experimental.pallas import tpu as pltpu
from jax.sharding import PartitionSpec as P

NK = 256
STEPS = 4
SUB = 8
BLOCK = 128

time_step = 0.25
ridge_weight = 0.1
HIGHEST = lax.Precision.HIGHEST


def pieces(value):
    high = value.astype(jnp.bfloat16)
    rest = value - high.astype(jnp.float32)
    middle = rest.astype(jnp.bfloat16)
    low = (rest - middle.astype(jnp.float32)).astype(jnp.bfloat16)
    return high, middle, low


def basis_kernel(factors_ref, weights_ref, bias_ref, payoff_ref, fit_ref, basis_ref, sums_ref, packed_ref):
    @pl.when(pl.program_id(0) == 0)
    def _():
        high, middle, low = pieces(weights_ref[...])
        packed_ref[...] = jnp.concatenate([high, high, middle, high, middle, low], axis=1)
        sums_ref[...] = jnp.zeros_like(sums_ref)

    high, middle, low = pieces(factors_ref[...])
    packed_factors = jnp.concatenate([high, middle, high, low, middle, high], axis=0)
    raised = jnp.dot(packed_ref[...], packed_factors, preferred_element_type=jnp.float32)
    basis = jnp.tanh(raised + bias_ref[...]).astype(jnp.bfloat16)
    basis_ref[...] = basis
    fit = fit_ref[...].astype(jnp.bfloat16)
    picked = basis * fit
    contract = (((1,), (1,)), ((), ()))
    functions = basis.shape[0]
    sums_ref[0:functions, :] += lax.dot_general(
        basis, picked, contract, preferred_element_type=jnp.float32
    )
    cash = jnp.broadcast_to(payoff_ref[...], (2 * SUB, basis.shape[1]))
    moment = lax.dot_general(cash, picked, contract, preferred_element_type=jnp.float32)
    sums_ref[functions : functions + SUB, :] += moment[0:SUB]


def basis_and_sums(factors, basis_w, basis_bias, payoff, in_fit):
    rank, functions = basis_w.shape
    paths = factors.shape[1]
    tile = min(1024, paths)
    return pl.pallas_call(
        basis_kernel,
        grid=(paths // tile,),
        in_specs=[
            pl.BlockSpec((rank, tile), lambda i: (0, i)),
            pl.BlockSpec((functions, rank), lambda i: (0, 0)),
            pl.BlockSpec((functions, 1), lambda i: (0, 0)),
            pl.BlockSpec((1, tile), lambda i: (0, i)),
            pl.BlockSpec((1, tile), lambda i: (0, i)),
        ],
        out_specs=[
            pl.BlockSpec((functions, tile), lambda i: (0, i)),
            pl.BlockSpec((functions + SUB, functions), lambda i: (0, 0)),
        ],
        out_shape=[
            jax.ShapeDtypeStruct((functions, paths), jnp.bfloat16),
            jax.ShapeDtypeStruct((functions + SUB, functions), jnp.float32),
        ],
        scratch_shapes=[pltpu.VMEM((functions, 6 * rank), jnp.bfloat16)],
        cost_estimate=pl.CostEstimate(
            flops=2 * functions * paths * (6 * rank + functions),
            bytes_accessed=functions * paths * 2,
            transcendentals=functions * paths,
        ),
        name="basis_sums",
    )(factors, basis_w.T, basis_bias[:, None], payoff[None, :], in_fit[None, :])


def sweep_block(tile_ref):
    size = tile_ref.shape[0]
    rows = lax.broadcasted_iota(jnp.int32, (SUB, size), 0)
    lanes = lax.broadcasted_iota(jnp.int32, (SUB, size), 1)
    all_lanes = lax.broadcasted_iota(jnp.int32, (size, size), 1)
    for start in range(0, size, SUB):
        whole = tile_ref[...]
        columns = [
            jnp.broadcast_to(whole[:, start + c : start + c + 1], (size, size)) for c in range(SUB)
        ]
        pivots = [columns[c][start : start + SUB] for c in range(SUB)]
        strip = whole[start : start + SUB]
        inside = (lanes >= start) & (lanes < start + SUB)
        strip = jnp.where(inside, jnp.where(lanes - start == rows, 1.0, 0.0), strip)
        for j in range(SUB):
            inverse = 1.0 / pivots[j][j : j + 1]
            chosen = strip[j : j + 1] * inverse
            strip = jnp.where(rows == j, chosen, strip - pivots[j] * chosen)
            for c in range(j + 1, SUB):
                moved = pivots[c][j : j + 1] * inverse
                pivots[c] = jnp.where(rows == j, moved, pivots[c] - pivots[j] * moved)
        inside_all = (all_lanes >= start) & (all_lanes < start + SUB)
        updated = jnp.where(inside_all, 0.0, whole)
        for c in range(SUB):
            updated = updated - columns[c] * strip[c : c + 1]
        tile_ref[...] = updated
        tile_ref[start : start + SUB, :] = strip


def solve_kernel(scale, sums_ref, out_ref, system_ref, moment_ref, inverse_ref, reduced_ref, tile_ref):
    size = system_ref.shape[0]
    row_ids = lax.broadcasted_iota(jnp.int32, (size, size), 0)
    lane_ids = lax.broadcasted_iota(jnp.int32, (size, size), 1)
    system_ref[...] = sums_ref[0:size, :] * scale + jnp.where(row_ids == lane_ids, ridge_weight, 0.0)
    moment_ref[...] = sums_ref[size : size + SUB, :] * scale
    strip_lanes = lax.broadcasted_iota(jnp.int32, (BLOCK, size), 1)

    def eliminate(k, carry):
        here = pl.ds(pl.multiple_of(k * BLOCK, BLOCK), BLOCK)
        tile_ref[...] = system_ref[here, here]
        sweep_block(tile_ref)
        inverse = tile_ref[...]
        inverse_ref[here, :] = inverse
        right = jnp.where(strip_lanes >= (k + 1) * BLOCK, system_ref[here, :], 0.0)
        reduced = jnp.dot(inverse, right, preferred_element_type=jnp.float32, precision=HIGHEST)
        reduced_ref[here, :] = reduced
        system_ref[...] -= jnp.dot(
            system_ref[:, here], reduced, preferred_element_type=jnp.float32, precision=HIGHEST
        )
        moment_ref[...] -= jnp.dot(
            moment_ref[:, here], reduced, preferred_element_type=jnp.float32, precision=HIGHEST
        )
        return carry

    blocks = size // BLOCK
    lax.fori_loop(0, blocks, eliminate, 0)
    out_ref[...] = jnp.zeros_like(out_ref)

    def substitute(step, carry):
        k = blocks - 1 - step
        here = pl.ds(pl.multiple_of(k * BLOCK, BLOCK), BLOCK)
        known = lax.dot_general(
            out_ref[...],
            reduced_ref[here, :],
            (((1,), (1,)), ((), ())),
            preferred_element_type=jnp.float32,
            precision=HIGHEST,
        )
        out_ref[:, here] = (
            jnp.dot(
                moment_ref[:, here],
                inverse_ref[here, :],
                preferred_element_type=jnp.float32,
                precision=HIGHEST,
            )
            - known
        )
        return carry

    lax.fori_loop(0, blocks, substitute, 0)


def solve_coefficients(sums, path_count):
    size = sums.shape[1]
    return pl.pallas_call(
        functools.partial(solve_kernel, 1.0 / path_count),
        in_specs=[pl.BlockSpec(memory_space=pltpu.VMEM)],
        out_specs=pl.BlockSpec(memory_space=pltpu.VMEM),
        out_shape=jax.ShapeDtypeStruct((SUB, size), jnp.float32),
        scratch_shapes=[
            pltpu.VMEM((size, size), jnp.float32),
            pltpu.VMEM((SUB, size), jnp.float32),
            pltpu.VMEM((size, BLOCK), jnp.float32),
            pltpu.VMEM((size, size), jnp.float32),
            pltpu.VMEM((BLOCK, BLOCK), jnp.float32),
        ],
        cost_estimate=pl.CostEstimate(
            flops=20_000_000_000, bytes_accessed=sums.size * 4, transcendentals=0
        ),
        name="solve",
    )(sums)


def adjoint_kernel(
    whole_ref, own_ref, shocks_ref, value_ref, exercise_ref, bucket_ref, powers_ref, basket_ref,
    delta_ref, surface_ref, split_ref,
):
    rows = own_ref.shape[0]
    tile = own_ref.shape[1]

    @pl.when(pl.program_id(0) == 0)
    def _():
        high, middle, _ = pieces(powers_ref[...])
        split_ref[0] = high
        split_ref[1] = middle
        surface_ref[...] = jnp.zeros_like(surface_ref)

    whole = whole_ref[...]
    start = own_ref[...].astype(jnp.float32)
    gains = [
        exercise_ref[date : date + 1, :].astype(jnp.float32) * value_ref[...] for date in range(STEPS)
    ]
    strikes = lax.broadcasted_iota(jnp.int32, (NK, tile), 0)
    total = jnp.zeros(surface_ref.shape, jnp.float32)
    for date in range(STEPS - 1, -1, -1):
        power = STEPS - 1 - date
        part = pl.ds(power * rows, rows)
        adjoint = (
            start
            + jnp.dot(split_ref[0, part, :], whole, preferred_element_type=jnp.float32)
            + jnp.dot(split_ref[1, part, :], whole, preferred_element_type=jnp.float32)
        )
        for later in range(date, STEPS):
            adjoint = adjoint + basket_ref[:, later - date : later - date + 1] * gains[later]
        if date == 0:
            delta_ref[...] = adjoint
        vega = (adjoint * shocks_ref[date].astype(jnp.float32)).astype(jnp.bfloat16)
        one_hot = jnp.where(bucket_ref[date : date + 1, :] == strikes, 1.0, 0.0).astype(jnp.bfloat16)
        total = total + lax.dot_general(
            vega, one_hot, (((1,), (1,)), ((), ())), preferred_element_type=jnp.float32
        )
    surface_ref[...] += total


def adjoint_and_surface(whole, own, shocks, value, exercise, bucket, powers, baskets):
    stocks, paths = whole.shape
    rows = own.shape[0]
    tile = min(1024, paths)
    return pl.pallas_call(
        adjoint_kernel,
        grid=(paths // tile,),
        in_specs=[
            pl.BlockSpec((stocks, tile), lambda i: (0, i)),
            pl.BlockSpec((rows, tile), lambda i: (0, i)),
            pl.BlockSpec((STEPS, rows, tile), lambda i: (0, 0, i)),
            pl.BlockSpec((1, tile), lambda i: (0, i)),
            pl.BlockSpec((STEPS, tile), lambda i: (0, i)),
            pl.BlockSpec((STEPS, tile), lambda i: (0, i)),
            pl.BlockSpec((STEPS * rows, stocks), lambda i: (0, 0)),
            pl.BlockSpec((rows, STEPS), lambda i: (0, 0)),
        ],
        out_specs=[
            pl.BlockSpec((rows, tile), lambda i: (0, i)),
            pl.BlockSpec((rows, NK), lambda i: (0, 0)),
        ],
        out_shape=[
            jax.ShapeDtypeStruct((rows, paths), jnp.float32),
            jax.ShapeDtypeStruct((rows, NK), jnp.float32),
        ],
        scratch_shapes=[pltpu.VMEM((2, STEPS * rows, stocks), jnp.bfloat16)],
        cost_estimate=pl.CostEstimate(
            flops=4 * STEPS * rows * paths * (stocks + NK),
            bytes_accessed=paths * (2 * stocks + 14 * rows),
            transcendentals=0,
        ),
        name="adjoint_surface",
    )(whole, own, shocks, value, exercise, bucket, powers, baskets)


def transition_powers(corr_gen, basket, offset, rows):
    step = time_step * corr_gen.astype(jnp.float32)
    own_step = lax.dynamic_slice_in_dim(step, offset, rows, 0)
    own_basket = lax.dynamic_slice_in_dim(basket, offset, rows, 0)
    powers = [own_step]
    for _ in range(STEPS - 1):
        powers.append(powers[-1] + own_step + jnp.dot(powers[-1], step, precision=HIGHEST))
    baskets = [own_basket]
    for power in powers[:-1]:
        baskets.append(own_basket + jnp.dot(power, basket, precision=HIGHEST))
    return jnp.concatenate(powers, axis=0), jnp.stack(baskets, axis=1)


def per_device(
    prices, loadings, basis_w, basis_bias, payoff, in_fit, cotangent, shocks, corr_gen, basket,
    exercise, bucket,
):
    stock_count = lax.axis_size("stocks")
    local_stocks, local_paths = prices.shape
    share = local_paths // stock_count
    path_count = float(local_paths * lax.axis_size("paths"))
    index = lax.axis_index("stocks")
    partial_value = lax.dot_general(
        loadings, prices, (((0,), (0,)), ((), ())), preferred_element_type=jnp.float32
    )
    factors = lax.psum_scatter(partial_value, "stocks", scatter_dimension=1, tiled=True)
    payoff_own = lax.dynamic_slice_in_dim(payoff, index * share, share, 0)
    fit_own = lax.dynamic_slice_in_dim(in_fit, index * share, share, 0)
    basis, sums = basis_and_sums(factors, basis_w, basis_bias, payoff_own, fit_own)
    sums = lax.psum(sums, ("paths", "stocks"))
    sums, cotangent = lax.optimization_barrier((sums, cotangent))
    whole = lax.all_gather(cotangent, "stocks", axis=0, tiled=True)
    coefficients = solve_coefficients(sums, path_count)
    value_own = jnp.dot(coefficients, basis.astype(jnp.float32), precision=HIGHEST)[0:1]
    value = lax.all_gather(value_own, "stocks", axis=1, tiled=True)
    powers, baskets = transition_powers(corr_gen, basket, index * local_stocks, local_stocks)
    delta_out, partial_surface = adjoint_and_surface(
        whole, cotangent, shocks, value, exercise, bucket, powers, baskets
    )
    surface = lax.psum_scatter(partial_surface, "paths", scatter_dimension=1, tiled=True)
    return (delta_out, surface)


def solution(mesh):
    return jax.shard_map(
        per_device,
        mesh=mesh,
        in_specs=(
            P("stocks", "paths"),
            P("stocks", None),
            P(),
            P(),
            P("paths"),
            P("paths"),
            P("stocks", "paths"),
            P(None, "stocks", "paths"),
            P(),
            P(),
            P(None, "paths"),
            P(None, "paths"),
        ),
        out_specs=(P("stocks", "paths"), P("stocks", "paths")),
        check_vma=False,
    )
```

time: 550 us -> 346 us (0.63); the launches traced: 542 us -> 345 us
  local copies, waits for them, and re-layouts: 181 us -> 8.28 us
  waiting for transfers between devices: 86.6 us -> 245 us
  other arithmetic: 131 us -> 0.8 us
  matrix products: 96.1 us -> 7.61 us
  Pallas kernels: 0 us -> 60.7 us
  starting transfers between devices: 11.3 us -> 0.16 us
  blocking collectives: 18.5 us -> 9.11 us
    another operation x17 -> x1, other arithmetic: 118 us -> 0.06 us  [transition_powers(): return (jnp.concatenate(powers, axis=0), jnp.stack(baskets, axis=1))]
    psum x2 -> x1, waiting for transfers between devices: 32.8 us -> 131 us  [per_device(): sums = lax.psum(sums, ('paths', 'stocks'))]
    unnamed x43 -> x12, local copies, waits for them, and re-layouts: 94.4 us -> 3.98 us
    dot_general x12 -> x7, matrix products: 88.4 us -> 5.18 us  [the longest x1 3.93 us: per_device(): jnp.dot(coefficients, basis.astype(jnp.float32), precision=HIGHEST)[0:1]]
    pallas_call x0 -> x3, Pallas kernels: none -> 60.7 us  [the longest x1 29.3 us: adjoint_and_surface(): pl.pallas_call(adjoint_kernel, grid=(paths // tile,), in_specs=[pl.BlockS...]
    all_gather x0 -> x1, waiting for transfers between devices: none -> 49.8 us  [per_device(): whole = lax.all_gather(cotangent, 'stocks', axis=0, tiled=True)]
    all_to_all x2 -> x0, local copies, waits for them, and re-layouts: 36.8 us -> none  [the longest x1 32 us: per_device(): lax.all_to_all(stacked, 'stocks', split_axis=2, concat_axis=1, tiled=True)]
    concatenate x1 -> x0, local copies, waits for them, and re-layouts: 33.2 us -> none  [per_device(): stacked = jnp.concatenate([cotangent[None], shocks], axis=0)]
  transfers between devices with their start and end apart: 6 -> 4, of which waited for: 3 -> 4; matrix products, arithmetic and copies ran while one was open for 56% -> 3% of each run, Pallas kernels for 0% -> 7%
where the time goes in v1:
time: 346 us; the launch traced here: 345 us
  waiting for transfers between devices  245 us (71%)
  Pallas kernels  60.7 us (18%)
  between operations  13.9 us (4%)
  blocking collectives  9.11 us (3%)
  local copies, waits for them, and re-layouts  8.28 us (2%)
  matrix products  7.61 us (2%)
    psum x1, waiting for transfers between devices, per_device(): sums = lax.psum(sums, ('paths', 'stocks'))  131 us
    all_gather x1, waiting for transfers between devices, per_device(): whole = lax.all_gather(cotangent, 'stocks', axis=0, tiled=True)  49.8 us
    reduce_scatter x1, waiting for transfers between devices, per_device(): lax.psum_scatter(partial_value, 'stocks', scatter_dimension=1, tiled=True)  33.9 us
    unnamed x5, waiting for transfers between devices  30.8 us
    pallas_call x1, Pallas kernels, adjoint_and_surface(): pl.pallas_call(adjoint_kernel, grid=(paths // tile,), in_specs=[pl.BlockS...  29.3 us
    pallas_call x1, Pallas kernels, solve_coefficients(): pl.pallas_call(functools.partial(solve_kernel, 1.0 / path_count), in_spec...  24.2 us
    all_gather x1, blocking collectives, per_device(): value = lax.all_gather(value_own, 'stocks', axis=1, tiled=True)  9.11 us
    pallas_call x1, Pallas kernels, basis_and_sums(): pl.pallas_call(basis_kernel, grid=(paths // tile,), in_specs=[pl.BlockSpe...  7.17 us
  transfers between devices with their start and end apart: 4, of which 4 were waited for; matrix products, arithmetic and copies ran while one was open for 3% of the time, Pallas kernels for 7%

profile of v1, /device:TPU:0, one launch (start us, length us, event | category | flops | bytes accessed | tf_op | source)
XLA Modules:
  0.0 345.5 jit_solution(3040265586866973956)
XLA Ops:
  7.2 0.0 reduce-scatter.5.cloned.1.call-start
  7.2 1.5 copy-done
  8.8 2.4 fusion.14
  11.2 0.0 all-reduce.2.cloned.1.call-start
  11.3 0.7 dynamic_slice.12
  12.0 0.6 broadcast_in_dim.10.payoff_ref
  12.6 1.3 dynamic_slice.13
  13.9 0.8 copy.27
  14.8 0.9 copy.28.bias_ref
  15.6 33.9 %reduce-scatter.5.cloned.1.call-done.factors_ref = f32[32,4096]{1,0:T(8,128)} async-done(((f32[32,16384]{1,0:T(8,128)}), f32[32,4096]{1,0:T(8,128)}) %reduce-scatter.5.cloned.1.call-update) | async-done | bytes 524304 | tf_op jit(solution)/shard_map/reduce_scatter | solution.py:288
  49.5 7.2 %basis_sums.1 = (bf16[512,4096]{1,0:T(8,128)(2,1)}, f32[520,512]{1,0:T(8,128)}) custom-call(f32[32,4096]{1,0:T(8,128)} %reduce-scatter.5.cloned.1.call-done.factors_ref, f32[512,32]{1,0:T(8,128)} %bitcast.47, f32[512,1]{1,0:T(8,128)} %copy.28.bias_ref, bf16[1,4096]{1,0:T(2,128)(2,1)} %broadcast_in_dim.10.payoff_ref, s32[1,4096]{1,0:T(1,128)} %bitcast.51), custom_call_target="tpu_custom_call" | custom-call | flops 2952790016 | bytes 4194304 | tf_op jit(solution)/shard_map/basis_sums/pallas_call | solution.py:56
  56.7 0.0 all-reduce.2.cloned.1.call-update
  56.7 0.0 all-gather.2.cloned.1.call-start
  56.7 130.5 %all-reduce.2.cloned.1.call-done.sums_ref = f32[520,512]{1,0:T(8,128)} async-done(((f32[520,512]{1,0:T(8,128)}), f32[520,512]{1,0:T(8,128)}) %all-reduce.2.cloned.1.call-update) | async-done | bytes 1064976 | tf_op jit(solution)/shard_map/psum | solution.py:292
  187.3 0.0 reduce-scatter.7.cloned.1.call-start
  187.4 0.1 dynamic-slice_bitcast_fusion
  187.5 0.1 fusion.1
  187.6 0.3 convolution_add_fusion.2
  187.9 0.1 fusion.3
  188.1 0.3 convolution_add_fusion.1
  188.4 0.1 fusion.5
  188.5 0.1 pad_maximum_fusion.1
  188.6 0.7 copy.29.basket_ref
  189.3 0.3 convolution_add_fusion
  189.5 0.7 pad_maximum_fusion.powers_ref
  190.2 24.2 %solve.1 = f32[8,512]{1,0:T(8,128)} custom-call(f32[520,512]{1,0:T(8,128)} %all-reduce.2.cloned.1.call-done.sums_ref), custom_call_target="tpu_custom_call" | custom-call | flops 20000000000 | bytes 1064960 | tf_op jit(solution)/shard_map/solve/pallas_call | solution.py:168
  214.4 3.9 %fusion.9 = f32[1,4096]{1,0:T(1,128)S(1)} fusion(bf16[512,4096]{1,0:T(8,128)(2,1)} %get-tuple-element.11, f32[8,512]{1,0:T(8,128)} %solve.1), kind=kOutput, calls=%fused_computation.17 | convolution fusion | flops 25165824 | bytes 4212736 | tf_op jit(solution)/shard_map/dot_general | solution.py:296
  218.3 9.1 %all_gather.7.value_ref = f32[1,16384]{1,0:T(1,128)} all-gather(f32[1,4096]{1,0:T(1,128)S(1)} %fusion.9), channel_id=1, replica_groups=mesh['paths'=8,'stocks'=4] {'stocks'}, dimensions={1}, use_global_device_ids=true | all-gather | bytes 81920 | tf_op jit(solution)/shard_map/all_gather | solution.py:297
  227.4 49.8 %all-gather.2.cloned.1.call-done.whole_ref = bf16[256,16384]{1,0:T(8,128)(2,1)} async-done(((bf16[64,16384]{1,0:T(8,128)(2,1)}), bf16[256,16384]{1,0:T(8,128)(2,1)}) %all-gather.2.cloned.1.call-update) | async-done | bytes 8388624 | tf_op jit(solution)/shard_map/all_gather | solution.py:294
  277.3 29.3 %adjoint_surface.1 = (f32[64,16384]{1,0:T(8,128)}, f32[64,256]{1,0:T(8,128)}) custom-call(bf16[256,16384]{1,0:T(8,128)(2,1)} %all-gather.2.cloned.1.call-done.whole_ref, bf16[64,16384]{1,0:T(8,128)(2,1)} %own_ref, bf16[4,64,16384]{2,1,0:T(8,128)(2,1)} %shocks_ref.1, f32[1,16384]{1,0:T(1,128)} %all_gather.7.value_ref, s32[4,16384]{1,0:T(4,128)} %exercise_ref.1, ...), custom_call_target="tpu_custom_call" | custom-call | flops 8589934592 | bytes 23068672 | tf_op jit(solution)/shard_map/adjoint_surface/pallas_call | solution.py:232
  306.6 1.6 copy.31
  308.2 30.7 %reduce-scatter.7.cloned.1.call-done = f32[32,64]{1,0:T(8,128)} async-done(((f32[256,64]{1,0:T(8,128)}), f32[32,64]{1,0:T(8,128)}) %reduce-scatter.7.cloned.1.call-update) | async-done | bytes 8208
  (14 shorter events, 0.1 us)
Async XLA Ops:
  7.2 1.6 copy-start
  7.2 42.3 %reduce-scatter.5.cloned.1.call-start = ((), (), s32[]{:S(2)}) async-start(), calls=%async_computation.2 | async-start | bytes 2621440 | tf_op jit(solution)/shard_map/reduce_scatter | solution.py:288
  11.2 2.7 copy-start.2
  11.2 3.6 %copy-start.4 = (f32[512]{0:T(512)S(1)}, f32[512]{0:T(512)}, u32[]{:S(2)}) copy-start(f32[512]{0:T(512)} %param.15) | copy-start | bytes 6148
  11.2 176.1 %all-reduce.2.cloned.1.call-start = ((), (), s32[]{:S(2)}) async-start(), calls=%async_computation.3 | async-start | bytes 2129920 | tf_op jit(solution)/shard_map/psum | solution.py:292
  56.6 130.7 %copy-start.3 = (f32[256]{0:T(256)S(1)}, f32[256]{0:T(256)}, u32[]{:S(2)}) copy-start(f32[256]{0:T(256)} %param.21) | copy-start | bytes 3076
  56.7 130.8 %copy-start.1 = (bf16[256,256]{1,0:T(8,128)(2,1)S(1)}, bf16[256,256]{1,0:T(8,128)(2,1)}, u32[]{:S(2)}) copy-start(bf16[256,256]{1,0:T(8,128)(2,1)} %param.20) | copy-start | bytes 393220
  56.7 220.6 %all-gather.2.cloned.1.call-start = ((), (), s32[]{:S(2)}) async-start(), calls=%async_computation.4 | async-start | bytes 10485760 | tf_op jit(solution)/shard_map/all_gather | solution.py:294
  187.3 151.6 %reduce-scatter.7.cloned.1.call-start = ((), (), s32[]{:S(2)}) async-start(), calls=%async_computation.5 | async-start | bytes 147456
Sparse Core Ops, SparseCore 0:
  11.5 37.9 reduce-scatter.4
  56.8 130.4 all-reduce.1
  189.1 88.0 all-gather.1
  308.3 30.5 reduce-scatter.6
